TPU v7x, 512 devices: a 4x2x32 block of a 4x8x32 slice. The times are simulated.
512 devices in a mesh: groups: 2 (over y), rows: 32 (over z), keys: 4 (over x), heads: 2 (over core).
Axes of the slice: x: 4, y: 2, z: 32, core: 2. Of those that a mesh axis runs over, the one named last changes fastest.
The devices are a block of a 4x8x32 slice.
Arguments:
- pair: bfloat16 [2048, 1024, 128], P(('groups', 'rows'), 'keys'), parts along dimension 0, may hold values from -6 to 6
- seq_length: int32 [2], P('groups'), parts along dimension 0, may hold values from 513 to 1024
- tile_counts: int32 [2048, 8], P(('groups', 'rows')), parts along dimension 0, may hold values from 0 to 128, as said below
- ln_gain: float32 [128], replicated, may hold values from 0.5 to 1.5
- w_query: bfloat16 [128, 128], P(None, 'heads'), may hold values from -8 to 8
- w_key: bfloat16 [128, 128], P(None, 'heads'), may hold values from -0.5 to 0.5
- w_value: bfloat16 [128, 128], P(None, 'heads'), may hold values from -0.5 to 0.5
- w_gate: bfloat16 [128, 128], P(None, 'heads'), may hold values from -0.5 to 0.5
- w_bias: bfloat16 [128, 4], P(None, 'heads'), may hold values from -1.5 to 1.5
- w_out: bfloat16 [128, 128], replicated, may hold values from -2 to 2
Outputs:
- update: bfloat16 [2048, 1024, 128], P(('groups', 'rows'), ('keys', 'heads')), parts along dimension 0
There are 2 independent parts, one for each index of `groups`. A program takes and returns all parts, laid end to end along the dimension named above; an argument that names none is the same for every part. Nothing has to cross between parts.
Inputs may be any that keep to these rules, and one draw needn't show every extreme that they name: `tile_counts`: for each row and each tile of 128 keys, how many of the tile's leading keys are valid; some rows have no valid key at all.
All inputs are finite; a program needn't handle non-finite values.
Results may differ from a plain program's by a relative error of at most 0.03.
The roundings to bfloat16 on the way count: a program that leaves them out, or rounds other values in their place, can miss the bound.
Values may be sent and summed in bfloat16 or wider, within the bound.
A program may use at most 128 MiB of HBM per device.

v0:
```python
import jax
import jax.numpy as jnp
from jax import lax
from jax.sharding import PartitionSpec as P

HEAD_DIM = 32
TILE = 128
norm_epsilon = 1e-05
masked_score = -1e30


def from_everyone(value, axis):
    peers = lax.axis_size(axis)
    return lax.all_to_all(
        jnp.broadcast_to(value[None], (peers, *value.shape)), axis, 0, 0, tiled=True
    )


def laid_out(tiles, dim):
    tiles = jnp.moveaxis(tiles, 0, dim)
    dims = tiles.shape
    return tiles.reshape(*dims[:dim], dims[dim] * dims[dim + 1], *dims[dim + 2 :])


def gathered_copies(value, axis, dim):
    tiles = from_everyone(value, axis)
    return laid_out(tiles, dim)


def sent_together(arrays, axis, dim, along):
    ends, at = ([], 0)
    for a in arrays[:-1]:
        at += a.shape[along]
        ends.append(at)
    both = jnp.concatenate(arrays, axis=along)
    return tuple(jnp.split(lax.all_gather(both, axis, axis=dim, tiled=True), ends, axis=along))


def exchange_in_groups(value, axis, split_dim, concat_dim, work, item_dim, out_dim):
    items = jax.tree.leaves(value)[0].shape[item_dim]
    count = 2 if items % 2 == 0 else 1
    done = []
    for k in range(count):
        group = jax.tree.map(
            lambda a: lax.slice_in_dim(
                a, k * (items // count), (k + 1) * (items // count), axis=item_dim
            ),
            value,
        )
        done.append(
            work(
                lax.all_to_all(
                    group, axis, split_axis=split_dim, concat_axis=concat_dim, tiled=True
                )
            )
        )
    return jax.tree.map(lambda *parts: jnp.concatenate(parts, axis=out_dim), *done)


def layer_norm(values, gain):
    center = values - jnp.mean(values, axis=-1, keepdims=True)
    spread = jnp.mean(center * center, axis=-1, keepdims=True)
    return center * lax.rsqrt(spread + norm_epsilon) * gain


def finish(row_sum, weighted):
    denom = jnp.maximum(row_sum, 1.0)
    result = weighted / denom[..., None]
    rows_dev, heads_dev, cols_dev, depth = result.shape
    result = jnp.transpose(result, (0, 2, 1, 3)).reshape(rows_dev, cols_dev, heads_dev * depth)
    return result.astype(jnp.bfloat16)


def per_device(
    pair, seq_length, tile_counts, ln_gain, w_query, w_key, w_value, w_gate, w_bias, w_out
):
    rows_dev, cols_dev, channels = pair.shape
    key_groups = lax.axis_size("keys")
    length_all = cols_dev * key_groups
    heads_dev = w_bias.shape[1]
    width_dev = heads_dev * HEAD_DIM
    normed = layer_norm(pair.astype(jnp.float32), ln_gain).astype(jnp.bfloat16)
    flat = normed.reshape(rows_dev * cols_dev, channels)
    queries = (
        (jnp.dot(flat, w_query, preferred_element_type=jnp.float32) * HEAD_DIM ** (-0.5))
        .astype(jnp.bfloat16)
        .reshape(rows_dev, cols_dev, heads_dev, HEAD_DIM)
    )
    keys_local = (
        jnp.dot(flat, w_key, preferred_element_type=jnp.float32)
        .astype(jnp.bfloat16)
        .reshape(rows_dev, cols_dev, heads_dev, HEAD_DIM)
    )
    values_local = (
        jnp.dot(flat, w_value, preferred_element_type=jnp.float32)
        .astype(jnp.bfloat16)
        .reshape(rows_dev, cols_dev, heads_dev, HEAD_DIM)
    )
    gate_act = jax.nn.sigmoid(jnp.dot(flat, w_gate, preferred_element_type=jnp.float32)).reshape(
        rows_dev, cols_dev, width_dev
    )
    bias_local = jnp.einsum("rkc,ch->hrk", normed, w_bias, preferred_element_type=jnp.float32)
    bias_rows = gathered_copies(bias_local.astype(jnp.bfloat16), "rows", 1).astype(bias_local.dtype)
    positions = jnp.arange(length_all, dtype=jnp.int32)
    allowed = (positions[None, :] < seq_length[0]) & (
        (positions % TILE)[None, :] < jnp.repeat(tile_counts, TILE, axis=1)
    )
    bias_turn = lax.all_to_all(
        bias_rows.astype(jnp.bfloat16), "keys", split_axis=1, concat_axis=2, tiled=True
    ).astype(bias_rows.dtype)
    initial = (
        jnp.full((rows_dev, heads_dev, cols_dev), masked_score, jnp.float32),
        jnp.zeros((rows_dev, heads_dev, cols_dev), jnp.float32),
        jnp.zeros((rows_dev, heads_dev, cols_dev, HEAD_DIM), jnp.float32),
    )
    piece_keys, piece_values = sent_together((keys_local, values_local), "keys", 1, 0)

    def one_tile(tile_index, state):
        row_max, row_sum, weighted = state
        offset = tile_index * TILE
        key_tile = lax.dynamic_slice_in_dim(piece_keys, offset, TILE, 1)
        value_tile = lax.dynamic_slice_in_dim(piece_values, offset, TILE, 1)
        tile_bias = lax.dynamic_slice_in_dim(bias_turn, offset, TILE, 2)
        shown = lax.dynamic_slice_in_dim(allowed, offset, TILE, 1)[:, None, None, :]
        scores = (
            jnp.einsum("rjhd,rkhd->rhjk", queries, key_tile, preferred_element_type=jnp.float32)
            + tile_bias[None]
        )
        scores = jnp.where(shown, scores, masked_score)
        new_max = jnp.maximum(row_max, jnp.max(scores, axis=-1))
        weights = jnp.where(shown, jnp.exp(scores - new_max[..., None]), 0.0)
        rescale = jnp.exp(row_max - new_max)
        row_sum = row_sum * rescale + jnp.sum(weights, axis=-1)
        weighted = weighted * rescale[..., None] + jnp.einsum(
            "rhjk,rkhd->rhjd",
            weights.astype(jnp.bfloat16),
            value_tile,
            preferred_element_type=jnp.float32,
        )
        return (new_max, row_sum, weighted)

    row_max, row_sum, weighted = lax.fori_loop(0, piece_keys.shape[1] // TILE, one_tile, initial)
    attended = finish(row_sum, weighted)
    attended = lax.optimization_barrier(attended).astype(jnp.float32)
    gated = (gate_act * attended).astype(jnp.bfloat16)

    def project(mixed):
        return jnp.einsum("rkc,cd->rkd", mixed, w_out, preferred_element_type=jnp.float32).astype(
            jnp.bfloat16
        )

    return exchange_in_groups(gated, "heads", 1, 2, project, 0, 0)


def solution(mesh):
    in_specs = (
        P(("groups", "rows"), "keys", None),
        P("groups"),
        P(("groups", "rows"), None),
        P(),
        P(None, "heads"),
        P(None, "heads"),
        P(None, "heads"),
        P(None, "heads"),
        P(None, "heads"),
        P(),
    )
    out_specs = P(("groups", "rows"), ("keys", "heads"), None)
    return jax.shard_map(
        per_device, mesh=mesh, in_specs=in_specs, out_specs=out_specs, check_vma=False
    )
```

profile of v0, /device:TPU:33, one launch (start us, length us, event | category | flops | bytes accessed | tf_op | source)
XLA Modules:
  0.0 321.6 jit_solution(10131734697609890808)
XLA Ops:
  21.3 46.3 %all-to-all-start = ((bf16[32,2,32,256]{3,2,1,0:T(8,128)(2,1)}), bf16[32,2,32,256]{3,2,1,0:T(8,128)(2,1)}, u32[]{:S(2)}, u32[]{:S(2)}) async-start(bf16[32,2,32,256]{3,2,1,0:T(8,128)(2,1)} %broadcast_in_dim.74), calls=%async_computation | async-start | bytes 2097152 | tf_op jit(solution)/shard_map/all_to_all | solution.py:14
  69.1 103.0 %all-to-all-done = bf16[32,2,32,256]{3,2,1,0:T(8,128)(2,1)} async-done(((bf16[32,2,32,256]{3,2,1,0:T(8,128)(2,1)}), bf16[32,2,32,256]{3,2,1,0:T(8,128)(2,1)}, u32[]{:S(2)}, u32[]{:S(2)}) %all-to-all-start) | async-done | bytes 1048608 | tf_op jit(solution)/shard_map/all_to_all | solution.py:14
  175.5 4.5 %all-to-all-start.1 = ((bf16[2,1024,256]{2,0,1:T(2,128)(2,1)}), bf16[2,1024,256]{2,0,1:T(2,128)(2,1)}, u32[]{:S(2)}, u32[]{:S(2)}) async-start(bf16[2,1024,256]{2,0,1:T(2,128)(2,1)} %copy.65), calls=%async_computation.1 | async-start | bytes 2097152 | tf_op jit(solution)/shard_map/all_to_all | solution.py:108
  183.4 10.9 %all-to-all-done.1 = bf16[2,1024,256]{2,0,1:T(2,128)(2,1)} async-done(((bf16[2,1024,256]{2,0,1:T(2,128)(2,1)}), bf16[2,1024,256]{2,0,1:T(2,128)(2,1)}, u32[]{:S(2)}, u32[]{:S(2)}) %all-to-all-start.1) | async-done | bytes 1048608 | tf_op jit(solution)/shard_map/all_to_all | solution.py:108
  197.7 6.4 %fusion.37 = (bf16[32,1024,2,32]{1,3,2,0:T(8,128)(2,1)}, bf16[32,1024,2,32]{1,3,2,0:T(8,128)(2,1)}) fusion(bf16[64,1024,2,32]{1,3,2,0:T(8,128)(2,1)} %all-gather.2.cloned.1.call-done), kind=kLoop, calls=%fused_computation.63 | loop fusion | bytes 16777216 | tf_op jit(solution)/shard_map/split | solution.py:36
  204.0 90.0 %while.18 = (s32[]{:T(128)}, f32[32,2,256]{2,1,0:T(2,128)S(1)}, f32[32,2,256]{2,1,0:T(2,128)S(1)}, f32[32,2,256,32]{2,3,1,0:T(8,128)S(1)}, pred[32,1024]{1,0:T(8...) while((s32[]{:T(128)}, f32[32,2,256]{2,1,0:T(2,128)S(1)}, ...), condition=%wide.region_5.6_spmd.clone, body=%wide.region_2.5_spmd.clone.sunk | while | flops 297353216 | bytes 33837260 | solution.py:142
  205.0 3.4 %fusion.62 = (f32[32,2,256]{2,1,0:T(2,128)S(1)}, f32[32,2,128,256]{3,2,1,0:T(8,128)S(1)}) fusion(f32[2,256,128]{1,2,0:T(8,128)S(1)} %constant_dynamic-slice_fusion.4, pred[32,128]{1,0:T(8,128)(4,1)S(1)} %constant_dynamic-slice_fusion.5, bf16[32,256,2,32]{1,3,2,0:T(8,128)(2,1)S(1)} %get-tuple-element.358, ...), kind=kOutput, calls=%fused_computation.3.clone.1 | convolution fusion | flops 140492800 | bytes 10293252 | tf_op jit(solution)/shard_map/while/body/eval_jaxpr/rjhd,rkhd->rhjk/dot_general | solution.py:126
  208.5 3.0 fusion.64
  211.6 3.6 %fusion.66 = f32[32,2,256,32]{2,3,1,0:T(8,128)S(1)} fusion(f32[32,2,256,32]{2,3,1,0:T(8,128)S(1)} %get-tuple-element.342, f32[32,2,128,256]{3,2,1,0:T(8,128)S(1)} %get-tuple-element.323, f32[32,2,256]{2,1,0:T(2,128)S(1)} %fusion.63, f32[2,256,128]{1,2,0:T(8,128)S(1)} %constant_dynamic-slice_fusion.4, ...), kind=kOutput, calls=%fused_computation.9.clone.1 | convolution fusion | flops 146276352 | bytes 13504517 | tf_op jit(solution)/shard_map/while/body/eval_jaxpr/rhjk,rkhd->rhjd/dot_general | solution.py:134
  216.3 3.4 %fusion.62 = (f32[32,2,256]{2,1,0:T(2,128)S(1)}, f32[32,2,128,256]{3,2,1,0:T(8,128)S(1)}) fusion(f32[2,256,128]{1,2,0:T(8,128)S(1)} %constant_dynamic-slice_fusion.4, pred[32,128]{1,0:T(8,128)(4,1)S(1)} %constant_dynamic-slice_fusion.5, bf16[32,256,2,32]{1,3,2,0:T(8,128)(2,1)S(1)} %get-tuple-element.358, ...), kind=kOutput, calls=%fused_computation.3.clone.1 | convolution fusion | flops 140492800 | bytes 10293252 | tf_op jit(solution)/shard_map/while/body/eval_jaxpr/rjhd,rkhd->rhjk/dot_general | solution.py:126
  219.7 3.0 fusion.64
  222.9 3.6 %fusion.66 = f32[32,2,256,32]{2,3,1,0:T(8,128)S(1)} fusion(f32[32,2,256,32]{2,3,1,0:T(8,128)S(1)} %get-tuple-element.342, f32[32,2,128,256]{3,2,1,0:T(8,128)S(1)} %get-tuple-element.323, f32[32,2,256]{2,1,0:T(2,128)S(1)} %fusion.63, f32[2,256,128]{1,2,0:T(8,128)S(1)} %constant_dynamic-slice_fusion.4, ...), kind=kOutput, calls=%fused_computation.9.clone.1 | convolution fusion | flops 146276352 | bytes 13504517 | tf_op jit(solution)/shard_map/while/body/eval_jaxpr/rhjk,rkhd->rhjd/dot_general | solution.py:134
  227.5 3.4 %fusion.62 = (f32[32,2,256]{2,1,0:T(2,128)S(1)}, f32[32,2,128,256]{3,2,1,0:T(8,128)S(1)}) fusion(f32[2,256,128]{1,2,0:T(8,128)S(1)} %constant_dynamic-slice_fusion.4, pred[32,128]{1,0:T(8,128)(4,1)S(1)} %constant_dynamic-slice_fusion.5, bf16[32,256,2,32]{1,3,2,0:T(8,128)(2,1)S(1)} %get-tuple-element.358, ...), kind=kOutput, calls=%fused_computation.3.clone.1 | convolution fusion | flops 140492800 | bytes 10293252 | tf_op jit(solution)/shard_map/while/body/eval_jaxpr/rjhd,rkhd->rhjk/dot_general | solution.py:126
  231.0 3.0 fusion.64
  234.1 3.6 %fusion.66 = f32[32,2,256,32]{2,3,1,0:T(8,128)S(1)} fusion(f32[32,2,256,32]{2,3,1,0:T(8,128)S(1)} %get-tuple-element.342, f32[32,2,128,256]{3,2,1,0:T(8,128)S(1)} %get-tuple-element.323, f32[32,2,256]{2,1,0:T(2,128)S(1)} %fusion.63, f32[2,256,128]{1,2,0:T(8,128)S(1)} %constant_dynamic-slice_fusion.4, ...), kind=kOutput, calls=%fused_computation.9.clone.1 | convolution fusion | flops 146276352 | bytes 13504517 | tf_op jit(solution)/shard_map/while/body/eval_jaxpr/rhjk,rkhd->rhjd/dot_general | solution.py:134
  238.8 3.4 %fusion.62 = (f32[32,2,256]{2,1,0:T(2,128)S(1)}, f32[32,2,128,256]{3,2,1,0:T(8,128)S(1)}) fusion(f32[2,256,128]{1,2,0:T(8,128)S(1)} %constant_dynamic-slice_fusion.4, pred[32,128]{1,0:T(8,128)(4,1)S(1)} %constant_dynamic-slice_fusion.5, bf16[32,256,2,32]{1,3,2,0:T(8,128)(2,1)S(1)} %get-tuple-element.358, ...), kind=kOutput, calls=%fused_computation.3.clone.1 | convolution fusion | flops 140492800 | bytes 10293252 | tf_op jit(solution)/shard_map/while/body/eval_jaxpr/rjhd,rkhd->rhjk/dot_general | solution.py:126
  242.2 3.0 fusion.64
  245.4 3.6 %fusion.66 = f32[32,2,256,32]{2,3,1,0:T(8,128)S(1)} fusion(f32[32,2,256,32]{2,3,1,0:T(8,128)S(1)} %get-tuple-element.342, f32[32,2,128,256]{3,2,1,0:T(8,128)S(1)} %get-tuple-element.323, f32[32,2,256]{2,1,0:T(2,128)S(1)} %fusion.63, f32[2,256,128]{1,2,0:T(8,128)S(1)} %constant_dynamic-slice_fusion.4, ...), kind=kOutput, calls=%fused_computation.9.clone.1 | convolution fusion | flops 146276352 | bytes 13504517 | tf_op jit(solution)/shard_map/while/body/eval_jaxpr/rhjk,rkhd->rhjd/dot_general | solution.py:134
  250.0 3.4 %fusion.62 = (f32[32,2,256]{2,1,0:T(2,128)S(1)}, f32[32,2,128,256]{3,2,1,0:T(8,128)S(1)}) fusion(f32[2,256,128]{1,2,0:T(8,128)S(1)} %constant_dynamic-slice_fusion.4, pred[32,128]{1,0:T(8,128)(4,1)S(1)} %constant_dynamic-slice_fusion.5, bf16[32,256,2,32]{1,3,2,0:T(8,128)(2,1)S(1)} %get-tuple-element.358, ...), kind=kOutput, calls=%fused_computation.3.clone.1 | convolution fusion | flops 140492800 | bytes 10293252 | tf_op jit(solution)/shard_map/while/body/eval_jaxpr/rjhd,rkhd->rhjk/dot_general | solution.py:126
  253.5 3.0 fusion.64
  256.6 3.6 %fusion.66 = f32[32,2,256,32]{2,3,1,0:T(8,128)S(1)} fusion(f32[32,2,256,32]{2,3,1,0:T(8,128)S(1)} %get-tuple-element.342, f32[32,2,128,256]{3,2,1,0:T(8,128)S(1)} %get-tuple-element.323, f32[32,2,256]{2,1,0:T(2,128)S(1)} %fusion.63, f32[2,256,128]{1,2,0:T(8,128)S(1)} %constant_dynamic-slice_fusion.4, ...), kind=kOutput, calls=%fused_computation.9.clone.1 | convolution fusion | flops 146276352 | bytes 13504517 | tf_op jit(solution)/shard_map/while/body/eval_jaxpr/rhjk,rkhd->rhjd/dot_general | solution.py:134
  261.3 3.4 %fusion.62 = (f32[32,2,256]{2,1,0:T(2,128)S(1)}, f32[32,2,128,256]{3,2,1,0:T(8,128)S(1)}) fusion(f32[2,256,128]{1,2,0:T(8,128)S(1)} %constant_dynamic-slice_fusion.4, pred[32,128]{1,0:T(8,128)(4,1)S(1)} %constant_dynamic-slice_fusion.5, bf16[32,256,2,32]{1,3,2,0:T(8,128)(2,1)S(1)} %get-tuple-element.358, ...), kind=kOutput, calls=%fused_computation.3.clone.1 | convolution fusion | flops 140492800 | bytes 10293252 | tf_op jit(solution)/shard_map/while/body/eval_jaxpr/rjhd,rkhd->rhjk/dot_general | solution.py:126
  264.7 3.0 fusion.64
  267.9 3.6 %fusion.66 = f32[32,2,256,32]{2,3,1,0:T(8,128)S(1)} fusion(f32[32,2,256,32]{2,3,1,0:T(8,128)S(1)} %get-tuple-element.342, f32[32,2,128,256]{3,2,1,0:T(8,128)S(1)} %get-tuple-element.323, f32[32,2,256]{2,1,0:T(2,128)S(1)} %fusion.63, f32[2,256,128]{1,2,0:T(8,128)S(1)} %constant_dynamic-slice_fusion.4, ...), kind=kOutput, calls=%fused_computation.9.clone.1 | convolution fusion | flops 146276352 | bytes 13504517 | tf_op jit(solution)/shard_map/while/body/eval_jaxpr/rhjk,rkhd->rhjd/dot_general | solution.py:134
  272.5 3.4 %fusion.62 = (f32[32,2,256]{2,1,0:T(2,128)S(1)}, f32[32,2,128,256]{3,2,1,0:T(8,128)S(1)}) fusion(f32[2,256,128]{1,2,0:T(8,128)S(1)} %constant_dynamic-slice_fusion.4, pred[32,128]{1,0:T(8,128)(4,1)S(1)} %constant_dynamic-slice_fusion.5, bf16[32,256,2,32]{1,3,2,0:T(8,128)(2,1)S(1)} %get-tuple-element.358, ...), kind=kOutput, calls=%fused_computation.3.clone.1 | convolution fusion | flops 140492800 | bytes 10293252 | tf_op jit(solution)/shard_map/while/body/eval_jaxpr/rjhd,rkhd->rhjk/dot_general | solution.py:126
  276.0 3.0 fusion.64
  279.1 3.6 %fusion.66 = f32[32,2,256,32]{2,3,1,0:T(8,128)S(1)} fusion(f32[32,2,256,32]{2,3,1,0:T(8,128)S(1)} %get-tuple-element.342, f32[32,2,128,256]{3,2,1,0:T(8,128)S(1)} %get-tuple-element.323, f32[32,2,256]{2,1,0:T(2,128)S(1)} %fusion.63, f32[2,256,128]{1,2,0:T(8,128)S(1)} %constant_dynamic-slice_fusion.4, ...), kind=kOutput, calls=%fused_computation.9.clone.1 | convolution fusion | flops 146276352 | bytes 13504517 | tf_op jit(solution)/shard_map/while/body/eval_jaxpr/rhjk,rkhd->rhjd/dot_general | solution.py:134
  283.8 3.4 %fusion.62 = (f32[32,2,256]{2,1,0:T(2,128)S(1)}, f32[32,2,128,256]{3,2,1,0:T(8,128)S(1)}) fusion(f32[2,256,128]{1,2,0:T(8,128)S(1)} %constant_dynamic-slice_fusion.4, pred[32,128]{1,0:T(8,128)(4,1)S(1)} %constant_dynamic-slice_fusion.5, bf16[32,256,2,32]{1,3,2,0:T(8,128)(2,1)S(1)} %get-tuple-element.358, ...), kind=kOutput, calls=%fused_computation.3.clone.1 | convolution fusion | flops 140492800 | bytes 10293252 | tf_op jit(solution)/shard_map/while/body/eval_jaxpr/rjhd,rkhd->rhjk/dot_general | solution.py:126
  287.2 3.0 fusion.64
  290.4 3.6 %fusion.66 = f32[32,2,256,32]{2,3,1,0:T(8,128)S(1)} fusion(f32[32,2,256,32]{2,3,1,0:T(8,128)S(1)} %get-tuple-element.342, f32[32,2,128,256]{3,2,1,0:T(8,128)S(1)} %get-tuple-element.323, f32[32,2,256]{2,1,0:T(2,128)S(1)} %fusion.63, f32[2,256,128]{1,2,0:T(8,128)S(1)} %constant_dynamic-slice_fusion.4, ...), kind=kOutput, calls=%fused_computation.9.clone.1 | convolution fusion | flops 146276352 | bytes 13504517 | tf_op jit(solution)/shard_map/while/body/eval_jaxpr/rhjk,rkhd->rhjd/dot_general | solution.py:134
  297.9 5.7 %all_to_all.50 = bf16[2,2,65536]{2,1,0:T(2,128)(2,1)S(1)} all-to-all(bf16[2,2,65536]{2,1,0:T(2,128)(2,1)S(1)} %reshape.73), channel_id=1, replica_groups=mesh['groups'=2,'rows'=32,'keys'=4,'heads'=2] {'heads'}, dimensions={0} | all-to-all | bytes 1048576 | tf_op jit(solution)/shard_map/all_to_all | solution.py:52
  307.1 4.2 %all_to_all.51 = bf16[2,2,65536]{2,1,0:T(2,128)(2,1)S(1)} all-to-all(bf16[2,2,65536]{2,1,0:T(2,128)(2,1)S(1)} %reshape.71), channel_id=1, replica_groups=mesh['groups'=2,'rows'=32,'keys'=4,'heads'=2] {'heads'}, dimensions={0} | all-to-all | bytes 1048576 | tf_op jit(solution)/shard_map/all_to_all | solution.py:52
  (116 shorter events, 45.6 us)
Async XLA Ops:
  6.5 306.4 %copy-start = (bf16[128,128]{1,0:T(8,128)(2,1)S(1)}, bf16[128,128]{1,0:T(8,128)(2,1)}, u32[]{:S(2)}) copy-start(bf16[128,128]{1,0:T(8,128)(2,1)} %param.21) | copy-start | bytes 98308
  6.6 2.4 copy-start.1
  6.6 4.8 %copy-start.9 = (f32[128]{0:T(128)S(1)}, f32[128]{0:T(128)}, u32[]{:S(2)}) copy-start(f32[128]{0:T(128)} %param.15) | copy-start | bytes 1540
  6.6 191.1 %all-gather.2.cloned.1.call-start = ((), (), s32[]{:S(2)}) async-start(), calls=%async_computation.4 | async-start | bytes 10485760 | tf_op jit(solution)/shard_map/all_gather | solution.py:36
  6.6 4.8 %copy-start.2 = (bf16[32,256,128]{2,1,0:T(8,128)(2,1)S(1)}, bf16[32,256,128]{2,1,0:T(8,128)(2,1)}, u32[]{:S(2)}) copy-start(bf16[32,256,128]{2,1,0:T(8,128)(2,1)} %param.12) | copy-start | bytes 6291460
  11.4 2.5 copy-start.5
  14.7 0.9 copy-start.6
  18.8 0.7 copy-start.10
  20.1 48.1 %copy-start.7 = (bf16[128,64]{0,1:T(8,128)(2,1)S(1)}, bf16[128,64]{0,1:T(8,128)(2,1)}, u32[]{:S(2)}) copy-start(bf16[128,64]{0,1:T(8,128)(2,1)} %param.16) | copy-start | bytes 49156
  21.3 150.9 %all-to-all-start = ((bf16[32,2,32,256]{3,2,1,0:T(8,128)(2,1)}), bf16[32,2,32,256]{3,2,1,0:T(8,128)(2,1)}, u32[]{:S(2)}, u32[]{:S(2)}) async-start(bf16[32,2,32,256]{3,2,1,0:T(8,128)(2,1)} %broadcast_in_dim.74), calls=%async_computation | async-start | bytes 2097152 | tf_op jit(solution)/shard_map/all_to_all | solution.py:14
  173.4 6.6 %copy-start.8 = (s32[32,8]{0,1:T(8,128)S(1)}, s32[32,8]{0,1:T(8,128)}, u32[]{:S(2)}) copy-start(s32[32,8]{0,1:T(8,128)} %param.14) | copy-start | bytes 3076
  175.5 18.8 %all-to-all-start.1 = ((bf16[2,1024,256]{2,0,1:T(2,128)(2,1)}), bf16[2,1024,256]{2,0,1:T(2,128)(2,1)}, u32[]{:S(2)}, u32[]{:S(2)}) async-start(bf16[2,1024,256]{2,0,1:T(2,128)(2,1)} %copy.65), calls=%async_computation.1 | async-start | bytes 2097152 | tf_op jit(solution)/shard_map/all_to_all | solution.py:108
  180.1 1.0 copy-start.11
  197.6 6.4 %copy-start.4 = (f32[32,2,256,32]{2,3,1,0:T(8,128)S(1)}, f32[32,2,256,32]{2,3,1,0:T(8,128)}, u32[]{:S(2)}) copy-start(f32[32,2,256,32]{2,3,1,0:T(8,128)} %custom-call.2) | copy-start | bytes 6291460
  294.0 1.6 copy-start.3
Sparse Core Ops, SparseCore 0:
  19.0 126.4 all-gather.1
where the time goes:
time: 323 us; the launch traced here: 322 us
  waiting for transfers between devices  114 us (35%)
  matrix products  62 us (19%)
  starting transfers between devices  50.8 us (16%)
  other arithmetic  36.3 us (11%)
  local copies, waits for them, and re-layouts  33.6 us (10%)
  between operations  14.5 us (4%)
  blocking collectives  9.84 us (3%)
    all_to_all x1, waiting for transfers between devices, from_everyone(): lax.all_to_all(jnp.broadcast_to(value[None], (peers, *value.shape)), axis...  103 us
    all_to_all x1, starting transfers between devices, from_everyone(): lax.all_to_all(jnp.broadcast_to(value[None], (peers, *value.shape)), axis...  46.3 us
    dot_general x8, matrix products, one_tile(): jnp.einsum('rhjk,rkhd->rhjd', weights.astype(jnp.bfloat16), value_tile, p...  28.9 us
    dot_general x8, matrix products, one_tile(): jnp.einsum('rjhd,rkhd->rhjk', queries, key_tile, preferred_element_type=j...  27 us
    reduce_sum x8, other arithmetic, one_tile(): row_sum = row_sum * rescale + jnp.sum(weights, axis=-1)  24 us
    all_to_all x1, waiting for transfers between devices, per_device(): lax.all_to_all(bias_rows.astype(jnp.bfloat16), 'keys', split_axis=1, conc...  10.9 us
    all_to_all x2, blocking collectives, exchange_in_groups(): lax.all_to_all(group, axis, split_axis=split_dim, concat_axis=concat_dim,...  9.84 us
    dynamic_slice x8, local copies, waits for them, and re-layouts, one_tile(): tile_bias = lax.dynamic_slice_in_dim(bias_turn, offset, TILE, 2)  7.84 us
  transfers between devices with their start and end apart: 3, of which 2 were waited for; matrix products, arithmetic and copies ran while one was open for 4% of the time, Pallas kernels for 0%

commit v1 on v0

--- a/solution.py
+++ b/solution.py
@@ -2,11 +2,24 @@
 import jax.numpy as jnp
 from jax import lax
 from jax.sharding import PartitionSpec as P
+from jax.lax import axis_index, ppermute, psum
 
 HEAD_DIM = 32
 TILE = 128
 norm_epsilon = 1e-05
 masked_score = -1e30
+
+
+def register_wall_all(message, d_out, x_in):
+    front = message.shape
+    mixed_arr = message.reshape(*front[:d_out], x_in, front[d_out] // x_in, *front[d_out + 1 :])
+    return jnp.moveaxis(mixed_arr, d_out, 0)
+
+
+def direct_tails(inner_x, in_dim):
+    inner_x = jnp.moveaxis(inner_x, 0, in_dim)
+    extra = inner_x.shape
+    return inner_x.reshape(*extra[:in_dim], extra[in_dim] * extra[in_dim + 1], *extra[in_dim + 2 :])
 
 
 def from_everyone(value, axis):
@@ -74,6 +87,20 @@
 def per_device(
     pair, seq_length, tile_counts, ln_gain, w_query, w_key, w_value, w_gate, w_bias, w_out
 ):
+
+    def _move_strips_all(page, axis_name, local_x, row_data):
+        n_now, arr_now = (psum(1, axis_name), axis_index(axis_name))
+        outcome_arr = register_wall_all(page, local_x, n_now)
+        state_now = outcome_arr
+        for h in tuple(range(1, n_now)):
+            ready, main = ((arr_now + h) % n_now, (arr_now - h) % n_now)
+            now = lax.dynamic_index_in_dim(outcome_arr, ready, 0)
+            y = ppermute(
+                now, axis_name, tuple(((dev_j, (dev_j + h) % n_now) for dev_j in range(n_now)))
+            )
+            state_now = lax.dynamic_update_slice_in_dim(state_now, y, main, axis=0)
+        return direct_tails(state_now, row_data)
+
     rows_dev, cols_dev, channels = pair.shape
     key_groups = lax.axis_size("keys")
     length_all = cols_dev * key_groups
@@ -105,9 +132,9 @@
     allowed = (positions[None, :] < seq_length[0]) & (
         (positions % TILE)[None, :] < jnp.repeat(tile_counts, TILE, axis=1)
     )
-    bias_turn = lax.all_to_all(
-        bias_rows.astype(jnp.bfloat16), "keys", split_axis=1, concat_axis=2, tiled=True
-    ).astype(bias_rows.dtype)
+    bias_turn = _move_strips_all(bias_rows.astype(jnp.bfloat16), "keys", 1, 2).astype(
+        bias_rows.dtype
+    )
     initial = (
         jnp.full((rows_dev, heads_dev, cols_dev), masked_score, jnp.float32),
         jnp.zeros((rows_dev, heads_dev, cols_dev), jnp.float32),

time: 323 us -> 325 us (level)
  waiting for transfers between devices: 114 us -> 104 us
  starting transfers between devices: 50.8 us -> 56.8 us
  local copies, waits for them, and re-layouts: 33.6 us -> 37.3 us
    all_to_all x1 -> x0, waiting for transfers between devices: 10.9 us -> none  [per_device(): lax.all_to_all(bias_rows.astype(jnp.bfloat16), 'keys', split_axis=1, conc...]
    ppermute x0 -> x3, starting transfers between devices: none -> 10.5 us  [_move_strips_all(): ppermute(now, axis_name, tuple(((dev_j, (dev_j + h) % n_now) for dev_j in...]
    dynamic_update_slice x0 -> x3, local copies, waits for them, and re-layouts: none -> 5.01 us  [_move_strips_all(): state_now = lax.dynamic_update_slice_in_dim(state_now, y, main, axis=0)]
    all_to_all x1 -> x0, starting transfers between devices: 4.5 us -> none  [per_device(): lax.all_to_all(bias_rows.astype(jnp.bfloat16), 'keys', split_axis=1, conc...]
    ppermute x0 -> x3, waiting for transfers between devices: none -> 3.64 us  [_move_strips_all(): ppermute(now, axis_name, tuple(((dev_j, (dev_j + h) % n_now) for dev_j in...]
  transfers between devices with their start and end apart: 3 -> 5, of which waited for: 2 -> 2; matrix products, arithmetic and copies ran while one was open for 4% -> 5% of each run, Pallas kernels for 0% -> 0%
where the time goes in v1:
time: 325 us; the launch traced here: 323 us
  waiting for transfers between devices  104 us (32%)
  matrix products  62 us (19%)
  starting transfers between devices  56.8 us (17%)
  other arithmetic  37.5 us (12%)
  local copies, waits for them, and re-layouts  37.3 us (11%)
  between operations  14.7 us (5%)
  blocking collectives  10.1 us (3%)
    all_to_all x1, waiting for transfers between devices, from_everyone(): lax.all_to_all(jnp.broadcast_to(value[None], (peers, *value.shape)), axis...  101 us
    all_to_all x1, starting transfers between devices, from_everyone(): lax.all_to_all(jnp.broadcast_to(value[None], (peers, *value.shape)), axis...  46.3 us
    dot_general x8, matrix products, one_tile(): jnp.einsum('rhjk,rkhd->rhjd', weights.astype(jnp.bfloat16), value_tile, p...  28.9 us
    dot_general x8, matrix products, one_tile(): jnp.einsum('rjhd,rkhd->rhjk', queries, key_tile, preferred_element_type=j...  27 us
    reduce_sum x8, other arithmetic, one_tile(): row_sum = row_sum * rescale + jnp.sum(weights, axis=-1)  24 us
    ppermute x3, starting transfers between devices, _move_strips_all(): ppermute(now, axis_name, tuple(((dev_j, (dev_j + h) % n_now) for dev_j in...  10.5 us
    all_to_all x2, blocking collectives, exchange_in_groups(): lax.all_to_all(group, axis, split_axis=split_dim, concat_axis=concat_dim,...  10.1 us
    dynamic_slice x8, local copies, waits for them, and re-layouts, one_tile(): tile_bias = lax.dynamic_slice_in_dim(bias_turn, offset, TILE, 2)  7.84 us
  transfers between devices with their start and end apart: 5, of which 2 were waited for; matrix products, arithmetic and copies ran while one was open for 5% of the time, Pallas kernels for 0%

profile of v1, /device:TPU:33, one launch (start us, length us, event | category | flops | bytes accessed | tf_op | source)
XLA Modules:
  0.0 323.3 jit_solution(5408615050249136512)
XLA Ops:
  21.3 46.3 %all-to-all-start = ((bf16[32,2,32,256]{3,2,1,0:T(8,128)(2,1)}), bf16[32,2,32,256]{3,2,1,0:T(8,128)(2,1)}, u32[]{:S(2)}, u32[]{:S(2)}) async-start(bf16[32,2,32,256]{3,2,1,0:T(8,128)(2,1)} %broadcast_in_dim.74), calls=%async_computation | async-start | bytes 2097152 | tf_op jit(solution)/shard_map/all_to_all | solution.py:27
  71.4 100.7 %all-to-all-done = bf16[32,2,32,256]{3,2,1,0:T(8,128)(2,1)} async-done(((bf16[32,2,32,256]{3,2,1,0:T(8,128)(2,1)}), bf16[32,2,32,256]{3,2,1,0:T(8,128)(2,1)}, u32[]{:S(2)}, u32[]{:S(2)}) %all-to-all-start) | async-done | bytes 1048608 | tf_op jit(solution)/shard_map/all_to_all | solution.py:27
  175.6 3.3 %collective-permute-start = (bf16[1,2,256,256]{3,2,0,1:T(8,128)(2,1)S(1)}, bf16[1,2,256,256]{3,2,0,1:T(8,128)(2,1)}, u32[]{:S(2)}, u32[]{:S(2)}) collective-permute-start(bf16[1,2,256,256]{3,2,0,1:T(8,128)(2,1)S(1)} %get-tuple-element.265), channel_id=1, source_target_pairs={{0,2},{2,4},{4,6},{6,0},{1,3},{3,5},{5,7},{7,1},{8,10},{10,12},{12... | collective-permute-start | bytes 786440 | tf_op jit(solution)/shard_map/ppermute | solution.py:98
  179.0 3.5 %collective-permute-start.2 = (bf16[1,2,256,256]{3,2,0,1:T(8,128)(2,1)S(1)}, bf16[1,2,256,256]{3,2,0,1:T(8,128)(2,1)}, u32[]{:S(2)}, u32[]{:S(2)}) collective-permute-start(bf16[1,2,256,256]{3,2,0,1:T(8,128)(2,1)S(1)} %get-tuple-element.263), channel_id=1, source_target_pairs={{0,6},{2,0},{4,2},{6,4},{1,7},{3,1},{5,3},{7,5},{8,14},{10,8},{12,... | collective-permute-start | bytes 786440 | tf_op jit(solution)/shard_map/ppermute | solution.py:98
  182.4 3.7 %collective-permute-start.1 = (bf16[1,2,256,256]{3,2,0,1:T(8,128)(2,1)S(1)}, bf16[1,2,256,256]{3,2,0,1:T(8,128)(2,1)}, u32[]{:S(2)}, u32[]{:S(2)}) collective-permute-start(bf16[1,2,256,256]{3,2,0,1:T(8,128)(2,1)S(1)} %get-tuple-element.264), channel_id=1, source_target_pairs={{0,4},{2,6},{4,0},{6,2},{1,5},{3,7},{5,1},{7,3},{8,12},{10,14},{12... | collective-permute-start | bytes 786440 | tf_op jit(solution)/shard_map/ppermute | solution.py:98
  189.0 3.6 %collective-permute-done.1 = bf16[1,2,256,256]{3,2,0,1:T(8,128)(2,1)} collective-permute-done((bf16[1,2,256,256]{3,2,0,1:T(8,128)(2,1)S(1)}, bf16[1,2,256,256]{3,2,0,1:T(8,128)(2,1)}, u32[]{:S(2)}, u32[]{:S(2)}) %collective-permute-start.1) | collective-permute-done | bytes 262176 | tf_op jit(solution)/shard_map/ppermute | solution.py:98
  199.2 6.4 %fusion.37 = (bf16[32,1024,2,32]{1,3,2,0:T(8,128)(2,1)}, bf16[32,1024,2,32]{1,3,2,0:T(8,128)(2,1)}) fusion(bf16[64,1024,2,32]{1,3,2,0:T(8,128)(2,1)} %all-gather.2.cloned.1.call-done), kind=kLoop, calls=%fused_computation.69 | loop fusion | bytes 16777216 | tf_op jit(solution)/shard_map/split | solution.py:49
  205.6 90.0 %while.18 = (s32[]{:T(128)}, f32[32,2,256]{2,1,0:T(2,128)S(1)}, f32[32,2,256]{2,1,0:T(2,128)S(1)}, f32[32,2,256,32]{2,3,1,0:T(8,128)S(1)}, pred[32,1024]{1,0:T(8...) while((s32[]{:T(128)}, f32[32,2,256]{2,1,0:T(2,128)S(1)}, ...), condition=%wide.region_5.6_spmd.clone, body=%wide.region_2.5_spmd.clone.sunk | while | flops 297353216 | bytes 33837260 | solution.py:169
  206.6 3.4 %fusion.62 = (f32[32,2,256]{2,1,0:T(2,128)S(1)}, f32[32,2,128,256]{3,2,1,0:T(8,128)S(1)}) fusion(f32[2,256,128]{1,2,0:T(8,128)S(1)} %constant_dynamic-slice_fusion.4, pred[32,128]{1,0:T(8,128)(4,1)S(1)} %constant_dynamic-slice_fusion.5, bf16[32,256,2,32]{1,3,2,0:T(8,128)(2,1)S(1)} %get-tuple-element.361, ...), kind=kOutput, calls=%fused_computation.3.clone.1 | convolution fusion | flops 140492800 | bytes 10293252 | tf_op jit(solution)/shard_map/while/body/eval_jaxpr/rjhd,rkhd->rhjk/dot_general | solution.py:153
  210.0 3.0 fusion.64
  213.2 3.6 %fusion.66 = f32[32,2,256,32]{2,3,1,0:T(8,128)S(1)} fusion(f32[32,2,256,32]{2,3,1,0:T(8,128)S(1)} %get-tuple-element.345, f32[32,2,128,256]{3,2,1,0:T(8,128)S(1)} %get-tuple-element.326, f32[32,2,256]{2,1,0:T(2,128)S(1)} %fusion.63, f32[2,256,128]{1,2,0:T(8,128)S(1)} %constant_dynamic-slice_fusion.4, ...), kind=kOutput, calls=%fused_computation.9.clone.1 | convolution fusion | flops 146276352 | bytes 13504517 | tf_op jit(solution)/shard_map/while/body/eval_jaxpr/rhjk,rkhd->rhjd/dot_general | solution.py:161
  217.8 3.4 %fusion.62 = (f32[32,2,256]{2,1,0:T(2,128)S(1)}, f32[32,2,128,256]{3,2,1,0:T(8,128)S(1)}) fusion(f32[2,256,128]{1,2,0:T(8,128)S(1)} %constant_dynamic-slice_fusion.4, pred[32,128]{1,0:T(8,128)(4,1)S(1)} %constant_dynamic-slice_fusion.5, bf16[32,256,2,32]{1,3,2,0:T(8,128)(2,1)S(1)} %get-tuple-element.361, ...), kind=kOutput, calls=%fused_computation.3.clone.1 | convolution fusion | flops 140492800 | bytes 10293252 | tf_op jit(solution)/shard_map/while/body/eval_jaxpr/rjhd,rkhd->rhjk/dot_general | solution.py:153
  221.3 3.0 fusion.64
  224.4 3.6 %fusion.66 = f32[32,2,256,32]{2,3,1,0:T(8,128)S(1)} fusion(f32[32,2,256,32]{2,3,1,0:T(8,128)S(1)} %get-tuple-element.345, f32[32,2,128,256]{3,2,1,0:T(8,128)S(1)} %get-tuple-element.326, f32[32,2,256]{2,1,0:T(2,128)S(1)} %fusion.63, f32[2,256,128]{1,2,0:T(8,128)S(1)} %constant_dynamic-slice_fusion.4, ...), kind=kOutput, calls=%fused_computation.9.clone.1 | convolution fusion | flops 146276352 | bytes 13504517 | tf_op jit(solution)/shard_map/while/body/eval_jaxpr/rhjk,rkhd->rhjd/dot_general | solution.py:161
  229.1 3.4 %fusion.62 = (f32[32,2,256]{2,1,0:T(2,128)S(1)}, f32[32,2,128,256]{3,2,1,0:T(8,128)S(1)}) fusion(f32[2,256,128]{1,2,0:T(8,128)S(1)} %constant_dynamic-slice_fusion.4, pred[32,128]{1,0:T(8,128)(4,1)S(1)} %constant_dynamic-slice_fusion.5, bf16[32,256,2,32]{1,3,2,0:T(8,128)(2,1)S(1)} %get-tuple-element.361, ...), kind=kOutput, calls=%fused_computation.3.clone.1 | convolution fusion | flops 140492800 | bytes 10293252 | tf_op jit(solution)/shard_map/while/body/eval_jaxpr/rjhd,rkhd->rhjk/dot_general | solution.py:153
  232.5 3.0 fusion.64
  235.7 3.6 %fusion.66 = f32[32,2,256,32]{2,3,1,0:T(8,128)S(1)} fusion(f32[32,2,256,32]{2,3,1,0:T(8,128)S(1)} %get-tuple-element.345, f32[32,2,128,256]{3,2,1,0:T(8,128)S(1)} %get-tuple-element.326, f32[32,2,256]{2,1,0:T(2,128)S(1)} %fusion.63, f32[2,256,128]{1,2,0:T(8,128)S(1)} %constant_dynamic-slice_fusion.4, ...), kind=kOutput, calls=%fused_computation.9.clone.1 | convolution fusion | flops 146276352 | bytes 13504517 | tf_op jit(solution)/shard_map/while/body/eval_jaxpr/rhjk,rkhd->rhjd/dot_general | solution.py:161
  240.3 3.4 %fusion.62 = (f32[32,2,256]{2,1,0:T(2,128)S(1)}, f32[32,2,128,256]{3,2,1,0:T(8,128)S(1)}) fusion(f32[2,256,128]{1,2,0:T(8,128)S(1)} %constant_dynamic-slice_fusion.4, pred[32,128]{1,0:T(8,128)(4,1)S(1)} %constant_dynamic-slice_fusion.5, bf16[32,256,2,32]{1,3,2,0:T(8,128)(2,1)S(1)} %get-tuple-element.361, ...), kind=kOutput, calls=%fused_computation.3.clone.1 | convolution fusion | flops 140492800 | bytes 10293252 | tf_op jit(solution)/shard_map/while/body/eval_jaxpr/rjhd,rkhd->rhjk/dot_general | solution.py:153
  243.8 3.0 fusion.64
  246.9 3.6 %fusion.66 = f32[32,2,256,32]{2,3,1,0:T(8,128)S(1)} fusion(f32[32,2,256,32]{2,3,1,0:T(8,128)S(1)} %get-tuple-element.345, f32[32,2,128,256]{3,2,1,0:T(8,128)S(1)} %get-tuple-element.326, f32[32,2,256]{2,1,0:T(2,128)S(1)} %fusion.63, f32[2,256,128]{1,2,0:T(8,128)S(1)} %constant_dynamic-slice_fusion.4, ...), kind=kOutput, calls=%fused_computation.9.clone.1 | convolution fusion | flops 146276352 | bytes 13504517 | tf_op jit(solution)/shard_map/while/body/eval_jaxpr/rhjk,rkhd->rhjd/dot_general | solution.py:161
  251.6 3.4 %fusion.62 = (f32[32,2,256]{2,1,0:T(2,128)S(1)}, f32[32,2,128,256]{3,2,1,0:T(8,128)S(1)}) fusion(f32[2,256,128]{1,2,0:T(8,128)S(1)} %constant_dynamic-slice_fusion.4, pred[32,128]{1,0:T(8,128)(4,1)S(1)} %constant_dynamic-slice_fusion.5, bf16[32,256,2,32]{1,3,2,0:T(8,128)(2,1)S(1)} %get-tuple-element.361, ...), kind=kOutput, calls=%fused_computation.3.clone.1 | convolution fusion | flops 140492800 | bytes 10293252 | tf_op jit(solution)/shard_map/while/body/eval_jaxpr/rjhd,rkhd->rhjk/dot_general | solution.py:153
  255.0 3.0 fusion.64
  258.2 3.6 %fusion.66 = f32[32,2,256,32]{2,3,1,0:T(8,128)S(1)} fusion(f32[32,2,256,32]{2,3,1,0:T(8,128)S(1)} %get-tuple-element.345, f32[32,2,128,256]{3,2,1,0:T(8,128)S(1)} %get-tuple-element.326, f32[32,2,256]{2,1,0:T(2,128)S(1)} %fusion.63, f32[2,256,128]{1,2,0:T(8,128)S(1)} %constant_dynamic-slice_fusion.4, ...), kind=kOutput, calls=%fused_computation.9.clone.1 | convolution fusion | flops 146276352 | bytes 13504517 | tf_op jit(solution)/shard_map/while/body/eval_jaxpr/rhjk,rkhd->rhjd/dot_general | solution.py:161
  262.8 3.4 %fusion.62 = (f32[32,2,256]{2,1,0:T(2,128)S(1)}, f32[32,2,128,256]{3,2,1,0:T(8,128)S(1)}) fusion(f32[2,256,128]{1,2,0:T(8,128)S(1)} %constant_dynamic-slice_fusion.4, pred[32,128]{1,0:T(8,128)(4,1)S(1)} %constant_dynamic-slice_fusion.5, bf16[32,256,2,32]{1,3,2,0:T(8,128)(2,1)S(1)} %get-tuple-element.361, ...), kind=kOutput, calls=%fused_computation.3.clone.1 | convolution fusion | flops 140492800 | bytes 10293252 | tf_op jit(solution)/shard_map/while/body/eval_jaxpr/rjhd,rkhd->rhjk/dot_general | solution.py:153
  266.3 3.0 fusion.64
  269.4 3.6 %fusion.66 = f32[32,2,256,32]{2,3,1,0:T(8,128)S(1)} fusion(f32[32,2,256,32]{2,3,1,0:T(8,128)S(1)} %get-tuple-element.345, f32[32,2,128,256]{3,2,1,0:T(8,128)S(1)} %get-tuple-element.326, f32[32,2,256]{2,1,0:T(2,128)S(1)} %fusion.63, f32[2,256,128]{1,2,0:T(8,128)S(1)} %constant_dynamic-slice_fusion.4, ...), kind=kOutput, calls=%fused_computation.9.clone.1 | convolution fusion | flops 146276352 | bytes 13504517 | tf_op jit(solution)/shard_map/while/body/eval_jaxpr/rhjk,rkhd->rhjd/dot_general | solution.py:161
  274.1 3.4 %fusion.62 = (f32[32,2,256]{2,1,0:T(2,128)S(1)}, f32[32,2,128,256]{3,2,1,0:T(8,128)S(1)}) fusion(f32[2,256,128]{1,2,0:T(8,128)S(1)} %constant_dynamic-slice_fusion.4, pred[32,128]{1,0:T(8,128)(4,1)S(1)} %constant_dynamic-slice_fusion.5, bf16[32,256,2,32]{1,3,2,0:T(8,128)(2,1)S(1)} %get-tuple-element.361, ...), kind=kOutput, calls=%fused_computation.3.clone.1 | convolution fusion | flops 140492800 | bytes 10293252 | tf_op jit(solution)/shard_map/while/body/eval_jaxpr/rjhd,rkhd->rhjk/dot_general | solution.py:153
  280.7 3.6 %fusion.66 = f32[32,2,256,32]{2,3,1,0:T(8,128)S(1)} fusion(f32[32,2,256,32]{2,3,1,0:T(8,128)S(1)} %get-tuple-element.345, f32[32,2,128,256]{3,2,1,0:T(8,128)S(1)} %get-tuple-element.326, f32[32,2,256]{2,1,0:T(2,128)S(1)} %fusion.63, f32[2,256,128]{1,2,0:T(8,128)S(1)} %constant_dynamic-slice_fusion.4, ...), kind=kOutput, calls=%fused_computation.9.clone.1 | convolution fusion | flops 146276352 | bytes 13504517 | tf_op jit(solution)/shard_map/while/body/eval_jaxpr/rhjk,rkhd->rhjd/dot_general | solution.py:161
  285.3 3.4 %fusion.62 = (f32[32,2,256]{2,1,0:T(2,128)S(1)}, f32[32,2,128,256]{3,2,1,0:T(8,128)S(1)}) fusion(f32[2,256,128]{1,2,0:T(8,128)S(1)} %constant_dynamic-slice_fusion.4, pred[32,128]{1,0:T(8,128)(4,1)S(1)} %constant_dynamic-slice_fusion.5, bf16[32,256,2,32]{1,3,2,0:T(8,128)(2,1)S(1)} %get-tuple-element.361, ...), kind=kOutput, calls=%fused_computation.3.clone.1 | convolution fusion | flops 140492800 | bytes 10293252 | tf_op jit(solution)/shard_map/while/body/eval_jaxpr/rjhd,rkhd->rhjk/dot_general | solution.py:153
  291.9 3.6 %fusion.66 = f32[32,2,256,32]{2,3,1,0:T(8,128)S(1)} fusion(f32[32,2,256,32]{2,3,1,0:T(8,128)S(1)} %get-tuple-element.345, f32[32,2,128,256]{3,2,1,0:T(8,128)S(1)} %get-tuple-element.326, f32[32,2,256]{2,1,0:T(2,128)S(1)} %fusion.63, f32[2,256,128]{1,2,0:T(8,128)S(1)} %constant_dynamic-slice_fusion.4, ...), kind=kOutput, calls=%fused_computation.9.clone.1 | convolution fusion | flops 146276352 | bytes 13504517 | tf_op jit(solution)/shard_map/while/body/eval_jaxpr/rhjk,rkhd->rhjd/dot_general | solution.py:161
  299.4 5.9 %all_to_all.41 = bf16[2,2,65536]{2,1,0:T(2,128)(2,1)S(1)} all-to-all(bf16[2,2,65536]{2,1,0:T(2,128)(2,1)S(1)} %reshape.76), channel_id=1, replica_groups=mesh['groups'=2,'rows'=32,'keys'=4,'heads'=2] {'heads'}, dimensions={0} | all-to-all | bytes 1048576 | tf_op jit(solution)/shard_map/all_to_all | solution.py:65
  308.8 4.2 %all_to_all.42 = bf16[2,2,65536]{2,1,0:T(2,128)(2,1)S(1)} all-to-all(bf16[2,2,65536]{2,1,0:T(2,128)(2,1)S(1)} %reshape.74), channel_id=1, replica_groups=mesh['groups'=2,'rows'=32,'keys'=4,'heads'=2] {'heads'}, dimensions={0} | all-to-all | bytes 1048576 | tf_op jit(solution)/shard_map/all_to_all | solution.py:65
  (122 shorter events, 56.6 us)
Async XLA Ops:
  6.5 308.2 %copy-start = (bf16[128,128]{1,0:T(8,128)(2,1)S(1)}, bf16[128,128]{1,0:T(8,128)(2,1)}, u32[]{:S(2)}) copy-start(bf16[128,128]{1,0:T(8,128)(2,1)} %param.21) | copy-start | bytes 98308
  6.6 2.4 copy-start.1
  6.6 4.8 %copy-start.9 = (f32[128]{0:T(128)S(1)}, f32[128]{0:T(128)}, u32[]{:S(2)}) copy-start(f32[128]{0:T(128)} %param.15) | copy-start | bytes 1540
  6.6 192.6 %all-gather.2.cloned.1.call-start = ((), (), s32[]{:S(2)}) async-start(), calls=%async_computation.3 | async-start | bytes 10485760 | tf_op jit(solution)/shard_map/all_gather | solution.py:49
  6.6 4.8 %copy-start.2 = (bf16[32,256,128]{2,1,0:T(8,128)(2,1)S(1)}, bf16[32,256,128]{2,1,0:T(8,128)(2,1)}, u32[]{:S(2)}) copy-start(bf16[32,256,128]{2,1,0:T(8,128)(2,1)} %param.12) | copy-start | bytes 6291460
  11.4 2.5 copy-start.5
  14.7 0.9 copy-start.6
  18.9 0.7 copy-start.10
  20.2 48.2 %copy-start.7 = (bf16[128,64]{0,1:T(8,128)(2,1)S(1)}, bf16[128,64]{0,1:T(8,128)(2,1)}, u32[]{:S(2)}) copy-start(bf16[128,64]{0,1:T(8,128)(2,1)} %param.16) | copy-start | bytes 49156
  21.3 150.9 %all-to-all-start = ((bf16[32,2,32,256]{3,2,1,0:T(8,128)(2,1)}), bf16[32,2,32,256]{3,2,1,0:T(8,128)(2,1)}, u32[]{:S(2)}, u32[]{:S(2)}) async-start(bf16[32,2,32,256]{3,2,1,0:T(8,128)(2,1)} %broadcast_in_dim.74), calls=%async_computation | async-start | bytes 2097152 | tf_op jit(solution)/shard_map/all_to_all | solution.py:27
  68.3 0.9 copy-start.11
  71.4 107.5 %copy-start.8 = (s32[32,8]{0,1:T(8,128)S(1)}, s32[32,8]{0,1:T(8,128)}, u32[]{:S(2)}) copy-start(s32[32,8]{0,1:T(8,128)} %param.14) | copy-start | bytes 3076
  175.6 11.7 %collective-permute-start = (bf16[1,2,256,256]{3,2,0,1:T(8,128)(2,1)S(1)}, bf16[1,2,256,256]{3,2,0,1:T(8,128)(2,1)}, u32[]{:S(2)}, u32[]{:S(2)}) collective-permute-start(bf16[1,2,256,256]{3,2,0,1:T(8,128)(2,1)S(1)} %get-tuple-element.265), channel_id=1, source_target_pairs={{0,2},{2,4},{4,6},{6,0},{1,3},{3,5},{5,7},{7,1},{8,10},{10,12},{12... | collective-permute-start | bytes 786440 | tf_op jit(solution)/shard_map/ppermute | solution.py:98
  179.0 15.3 %collective-permute-start.2 = (bf16[1,2,256,256]{3,2,0,1:T(8,128)(2,1)S(1)}, bf16[1,2,256,256]{3,2,0,1:T(8,128)(2,1)}, u32[]{:S(2)}, u32[]{:S(2)}) collective-permute-start(bf16[1,2,256,256]{3,2,0,1:T(8,128)(2,1)S(1)} %get-tuple-element.263), channel_id=1, source_target_pairs={{0,6},{2,0},{4,2},{6,4},{1,7},{3,1},{5,3},{7,5},{8,14},{10,8},{12,... | collective-permute-start | bytes 786440 | tf_op jit(solution)/shard_map/ppermute | solution.py:98
  182.4 10.1 %collective-permute-start.1 = (bf16[1,2,256,256]{3,2,0,1:T(8,128)(2,1)S(1)}, bf16[1,2,256,256]{3,2,0,1:T(8,128)(2,1)}, u32[]{:S(2)}, u32[]{:S(2)}) collective-permute-start(bf16[1,2,256,256]{3,2,0,1:T(8,128)(2,1)S(1)} %get-tuple-element.264), channel_id=1, source_target_pairs={{0,4},{2,6},{4,0},{6,2},{1,5},{3,7},{5,1},{7,3},{8,12},{10,14},{12... | collective-permute-start | bytes 786440 | tf_op jit(solution)/shard_map/ppermute | solution.py:98
  199.2 6.4 %copy-start.4 = (f32[32,2,256,32]{2,3,1,0:T(8,128)S(1)}, f32[32,2,256,32]{2,3,1,0:T(8,128)}, u32[]{:S(2)}) copy-start(f32[32,2,256,32]{2,3,1,0:T(8,128)} %custom-call.2) | copy-start | bytes 6291460
  295.6 1.6 copy-start.3
Sparse Core Ops, SparseCore 0:
  19.0 126.4 all-gather.1
